TPU v7x, 128 devices: a whole 4x4x4 slice. The times are simulated.
128 devices in a mesh: batch: 1, outer: 2 (over core), rows: 64 (over z, y, x).
Axes of the slice: x: 4, y: 4, z: 4, core: 2. Of those that a mesh axis runs over, the one named last changes fastest.
Arguments:
- a_mat: float32 [131072, 1024], P(('batch', 'outer', 'rows'))
Outputs:
- output 1: float32 [131072, 1024], P(('batch', 'outer', 'rows'))
- output 2: float32 [1024, 1024], P('batch')
All inputs are finite; a program needn't handle non-finite values.
Results may differ from a plain program's by a relative error of at most 0.001.
Values sent between devices are 32-bit elements.
A program may use at most 1 GiB of HBM per device.

v0:
```python
import jax
import jax.numpy as jnp
from jax import lax
from jax.sharding import PartitionSpec as P

PRECISION = lax.Precision.HIGHEST
GROUP_AXES = ("outer", "rows")


def gram_of(block):
    return lax.dot_general(block, block, (((0,), (0,)), ((), ())), precision=PRECISION, preferred_element_type=jnp.float32)


def right_solve(chol_low, block):
    return lax.linalg.triangular_solve(chol_low, block, left_side=False, lower=True, transpose_a=True)


def solution(mesh):
    row_spec = P(("batch", "outer", "rows"), None)

    def group_qr(a_block):
        chol_one = jnp.linalg.cholesky(lax.psum(gram_of(a_block), GROUP_AXES))
        q_first = right_solve(chol_one, a_block)
        chol_two = jnp.linalg.cholesky(lax.psum(gram_of(q_first), GROUP_AXES))
        q_block = right_solve(chol_two, q_first)
        r_block = lax.dot_general(chol_two, chol_one, (((0,), (1,)), ((), ())), precision=PRECISION, preferred_element_type=jnp.float32)
        return q_block, r_block

    return jax.shard_map(group_qr, mesh=mesh, in_specs=(row_spec,), out_specs=(row_spec, P("batch", None)), check_vma=False)
```

profile of v0, /device:TPU:1, one launch (start us, length us, event | category | flops | bytes accessed | tf_op | source)
XLA Modules:
  0.0 1119.3 jit_solution(1393403527359398807)
XLA Ops:
  7.2 17.8 %fusion.170 = f32[1024,1024]{0,1:T(8,128)} fusion(f32[1024,1024]{1,0:T(8,128)} %param.4), kind=kOutput, calls=%fused_computation.328 | convolution fusion | flops 12884901888 | bytes 8388608 | tf_op jit(solution)/shard_map/dot_general | solution.py:11
  25.1 158.6 %all-reduce.4.cloned.1.call-done = f32[1024,1024]{0,1:T(8,128)} async-done(((f32[1024,1024]{0,1:T(8,128)}), f32[1024,1024]{0,1:T(8,128)}) %all-reduce.4.cloned.1.call-update) | async-done | bytes 4194320 | tf_op jit(solution)/shard_map/psum | solution.py:22
  183.7 5.5 copy.4
  195.6 11.7 %cholesky.619 = f32[128,128]{1,0:T(8,128)S(1)} custom-call(f32[128,128]{1,0:T(8,128)S(1)} %cholesky.911), custom_call_target="Cholesky" | custom-call | tf_op jit(solution)/shard_map/jit(cholesky)/cholesky | solution.py:22
  207.4 9.8 custom-call.55
  223.6 12.1 %cholesky.638 = f32[128,128]{1,0:T(8,128)S(1)} custom-call(f32[128,128]{1,0:T(8,128)S(1)} %cholesky.915), custom_call_target="Cholesky" | custom-call | tf_op jit(solution)/shard_map/jit(cholesky)/cholesky | solution.py:22
  236.4 9.8 custom-call.56
  249.5 11.7 %cholesky.659 = f32[128,128]{1,0:T(8,128)S(1)} custom-call(f32[128,128]{1,0:T(8,128)S(1)} %cholesky.920), custom_call_target="Cholesky" | custom-call | tf_op jit(solution)/shard_map/jit(cholesky)/cholesky | solution.py:22
  262.5 9.8 custom-call.57
  275.8 11.8 %cholesky.678 = f32[128,128]{1,0:T(8,128)S(1)} custom-call(f32[128,128]{1,0:T(8,128)S(1)} %cholesky.925), custom_call_target="Cholesky" | custom-call | tf_op jit(solution)/shard_map/jit(cholesky)/cholesky | solution.py:22
  289.0 9.8 custom-call.58
  302.3 11.7 %cholesky.697 = f32[128,128]{1,0:T(8,128)S(1)} custom-call(f32[128,128]{1,0:T(8,128)S(1)} %cholesky.930), custom_call_target="Cholesky" | custom-call | tf_op jit(solution)/shard_map/jit(cholesky)/cholesky | solution.py:22
  315.3 10.0 custom-call.59
  328.6 11.7 %cholesky.716 = f32[128,128]{1,0:T(8,128)S(1)} custom-call(f32[128,128]{1,0:T(8,128)S(1)} %cholesky.935), custom_call_target="Cholesky" | custom-call | tf_op jit(solution)/shard_map/jit(cholesky)/cholesky | solution.py:22
  341.5 9.8 custom-call.60
  354.4 12.1 %cholesky.735 = f32[128,128]{1,0:T(8,128)S(1)} custom-call(f32[128,128]{1,0:T(8,128)S(1)} %cholesky.940), custom_call_target="Cholesky" | custom-call | tf_op jit(solution)/shard_map/jit(cholesky)/cholesky | solution.py:22
  367.8 9.8 custom-call.61
  380.2 11.7 %cholesky.752 = f32[128,128]{1,0:T(8,128)S(1)} custom-call(f32[128,128]{1,0:T(8,128)S(1)} %convolution_subtract_fusion.23), custom_call_target="Cholesky" | custom-call | tf_op jit(solution)/shard_map/jit(cholesky)/cholesky | solution.py:22
  398.9 4.9 fusion.3
  403.8 23.8 %while.4 = (s32[]{:T(128)}, f32[1024,1024]{1,0:T(8,128)}, s32[8,2]{0,1:T(2,128)S(1)}, f32[8,128,128]{2,1,0:T(8,128)S(1)}, s32[]{:T(128)}) while((s32[]{:T(128)}, f32[1024,1024]{1,0:T(8,128)}, s32[8,2]{0,1:T(2,128)S(1)}, f32[8,128,128]{2,1,0:T(8,128)S(1)}, s32[]{:T(128)}) %tuple.120), condition=%wide.while_cond, body=%wide.while_body.sunk | while | flops 2 | bytes 131189 | solution.py:15
  427.6 78.8 %custom-call.62 = f32[8,128,128]{1,2,0:T(8,128)S(1)} custom-call(f32[8,128,128]{2,1,0:T(8,128)S(1)} %get-tuple-element.18), custom_call_target="InvertDiagBlocksLowerTriangular" | custom-call | tf_op jit(solution)/shard_map/triangular_solve/custom-call.7 | solution.py:15
  519.1 4.6 fusion.50
  525.6 5.4 convolution_subtract_fusion.5
  531.8 6.2 convolution_subtract_fusion.3
  539.5 7.3 convolution_subtract_fusion.8
  548.2 15.1 %fusion.171 = f32[1024,1024]{0,1:T(8,128)} fusion(f32[1024,1024]{0,1:T(8,128)S(1)} %get-tuple-element.145), kind=kOutput, calls=%fused_computation.329 | convolution fusion | flops 12884901888 | bytes 8388608 | tf_op jit(solution)/shard_map/dot_general | solution.py:11
  563.4 153.7 %all-reduce.6.cloned.1.call-done = f32[1024,1024]{0,1:T(8,128)} async-done(((f32[1024,1024]{0,1:T(8,128)}), f32[1024,1024]{0,1:T(8,128)}) %all-reduce.6.cloned.1.call-update) | async-done | bytes 4194320 | tf_op jit(solution)/shard_map/psum | solution.py:24
  717.1 5.7 copy.6
  729.3 11.7 %cholesky.767 = f32[128,128]{1,0:T(8,128)S(1)} custom-call(f32[128,128]{1,0:T(8,128)S(1)} %cholesky.944), custom_call_target="Cholesky" | custom-call | tf_op jit(solution)/shard_map/jit(cholesky)/cholesky | solution.py:24
  741.7 9.8 custom-call.63
  758.7 11.8 %cholesky.786 = f32[128,128]{1,0:T(8,128)S(1)} custom-call(f32[128,128]{1,0:T(8,128)S(1)} %cholesky.948), custom_call_target="Cholesky" | custom-call | tf_op jit(solution)/shard_map/jit(cholesky)/cholesky | solution.py:24
  771.8 9.8 custom-call.64
  786.6 13.2 %cholesky.807 = f32[128,128]{1,0:T(8,128)} custom-call(f32[128,128]{1,0:T(8,128)} %cholesky.953), custom_call_target="Cholesky" | custom-call | tf_op jit(solution)/shard_map/jit(cholesky)/cholesky | solution.py:24
  802.0 11.3 %custom-call.65 = f32[1,128,128]{1,2,0:T(8,128)} custom-call(f32[1,128,128]{2,1,0:T(8,128)} %get-tuple-element.107), custom_call_target="InvertDiagBlocksLowerTriangular" | custom-call | tf_op jit(solution)/shard_map/jit(cholesky)/cholesky | solution.py:24
  817.6 12.5 %cholesky.826 = f32[128,128]{1,0:T(8,128)} custom-call(f32[128,128]{1,0:T(8,128)S(1)} %cholesky.958), custom_call_target="Cholesky" | custom-call | tf_op jit(solution)/shard_map/jit(cholesky)/cholesky | solution.py:24
  832.3 10.4 custom-call.66
  847.0 11.7 %cholesky.845 = f32[128,128]{1,0:T(8,128)S(1)} custom-call(f32[128,128]{1,0:T(8,128)S(1)} %cholesky.963), custom_call_target="Cholesky" | custom-call | tf_op jit(solution)/shard_map/jit(cholesky)/cholesky | solution.py:24
  860.0 10.2 custom-call.67
  873.5 11.7 %cholesky.864 = f32[128,128]{1,0:T(8,128)S(1)} custom-call(f32[128,128]{1,0:T(8,128)S(1)} %cholesky.968), custom_call_target="Cholesky" | custom-call | tf_op jit(solution)/shard_map/jit(cholesky)/cholesky | solution.py:24
  886.5 9.8 custom-call.68
  899.3 11.9 %cholesky.883 = f32[128,128]{1,0:T(8,128)S(1)} custom-call(f32[128,128]{1,0:T(8,128)S(1)} %cholesky.973), custom_call_target="Cholesky" | custom-call | tf_op jit(solution)/shard_map/jit(cholesky)/cholesky | solution.py:24
  912.5 9.8 custom-call.69
  925.0 11.7 %cholesky.900 = f32[128,128]{1,0:T(8,128)S(1)} custom-call(f32[128,128]{1,0:T(8,128)S(1)} %convolution_subtract_fusion.22), custom_call_target="Cholesky" | custom-call | tf_op jit(solution)/shard_map/jit(cholesky)/cholesky | solution.py:24
  943.0 19.9 %fusion.6 = f32[1024,1024]{1,0:T(8,128)} fusion(f32[1024,1024]{1,0:T(8,128)} %get-tuple-element.93, f32[1024,1024]{1,0:T(8,128)} %get-tuple-element.115, pred[]{:T(512)S(6)} %cholesky.905, pred[]{:T(512)S(6)} %cholesky.757), kind=kOutput, calls=%fused_computation.13 | convolution fusion | flops 12891193344 | bytes 12582914 | tf_op jit(solution)/shard_map/dot_general | solution.py:26
  962.9 4.9 fusion.5
  968.6 28.3 %while.5 = (s32[]{:T(128)}, f32[1024,1024]{1,0:T(8,128)}, s32[8,2]{0,1:T(2,128)S(1)}, f32[8,128,128]{2,1,0:T(8,128)}, s32[]{:T(128)}) while((s32[]{:T(128)}, f32[1024,1024]{1,0:T(8,128)}, s32[8,2]{0,1:T(2,128)S(1)}, f32[8,128,128]{2,1,0:T(8,128)}, s32[]{:T(128)}) %tuple.130), condition=%wide.while_cond.clone, body=%wide.while_body.clone.sunk | while | flops 2 | bytes 132205 | solution.py:15
  996.9 80.3 %custom-call.70 = f32[8,128,128]{1,2,0:T(8,128)} custom-call(f32[8,128,128]{2,1,0:T(8,128)} %get-tuple-element.19), custom_call_target="InvertDiagBlocksLowerTriangular" | custom-call | tf_op jit(solution)/shard_map/triangular_solve/custom-call.7 | solution.py:15
  1106.6 5.3 copy.7
  (177 shorter events, 189.3 us)
Async XLA Ops:
  7.2 176.5 %all-reduce.4.cloned.1.call-start = ((), (), s32[]{:S(2)}) async-start(), calls=%async_computation | async-start | bytes 8388608 | tf_op jit(solution)/shard_map/psum | solution.py:22
  25.0 692.1 %all-reduce.6.cloned.1.call-start = ((), (), s32[]{:S(2)}) async-start(), calls=%async_computation.1 | async-start | bytes 8388608 | tf_op jit(solution)/shard_map/psum | solution.py:24
  193.6 2.0 copy-start.1
  506.4 24.7 %copy-start.8 = (f32[8,128,128]{1,2,0:T(8,128)}, f32[8,128,128]{1,2,0:T(8,128)S(1)}, u32[]{:S(2)}) copy-start(f32[8,128,128]{1,2,0:T(8,128)S(1)} %custom-call.62) | copy-start | bytes 1572868
  506.4 4.8 copy-start.2
  519.1 12.0 %copy-start.3 = (f32[1024,128]{0,1:T(8,128)}, f32[1024,128]{0,1:T(8,128)S(1)}, u32[]{:S(2)}) copy-start(f32[1024,128]{0,1:T(8,128)S(1)} %get-tuple-element.141) | copy-start | bytes 1572868
  727.2 2.0 copy-start
  758.0 0.8 copy-start.5
  1077.1 3.9 copy-start.7
  1081.0 4.7 copy-start.4
  1084.2 5.2 copy-start.6
Sparse Core Ops, SparseCore 0:
  25.1 158.4 all-reduce.3
  563.5 153.5 all-reduce.5
where the time goes:
time: 1130 us; the launch traced here: 1120 us
  other arithmetic  529 us (47%)
  waiting for transfers between devices  312 us (28%)
  matrix products  173 us (15%)
  local copies, waits for them, and re-layouts  79.9 us (7%)
  between operations  25.1 us (2%)
    another operation x31, other arithmetic, group_qr(): chol_two = jnp.linalg.cholesky(lax.psum(gram_of(q_first), GROUP_AXES))  179 us
    another operation x30, other arithmetic, group_qr(): chol_one = jnp.linalg.cholesky(lax.psum(gram_of(a_block), GROUP_AXES))  173 us
    another operation x5, other arithmetic, right_solve(): lax.linalg.triangular_solve(chol_low, block, left_side=False, lower=True,...  169 us
    psum x1, waiting for transfers between devices, group_qr(): chol_one = jnp.linalg.cholesky(lax.psum(gram_of(a_block), GROUP_AXES))  159 us
    psum x1, waiting for transfers between devices, group_qr(): chol_two = jnp.linalg.cholesky(lax.psum(gram_of(q_first), GROUP_AXES))  154 us
    another operation x30, matrix products, right_solve(): lax.linalg.triangular_solve(chol_low, block, left_side=False, lower=True,...  71 us
    another operation x51, local copies, waits for them, and re-layouts, right_solve(): lax.linalg.triangular_solve(chol_low, block, left_side=False, lower=True,...  52.8 us
    dot_general x2, matrix products, gram_of(): lax.dot_general(block, block, (((0,), (0,)), ((), ())), precision=PRECISI...  32.9 us
  transfers between devices with their start and end apart: 2, of which 2 were waited for; matrix products, arithmetic and copies ran while one was open for 0% of the time, Pallas kernels for 0%

commit v1 on v0

v1 whole, which is shorter than its diff:
```python
import jax
import jax.numpy as jnp
from jax import lax
from jax.experimental import pallas as pl
from jax.experimental.pallas import tpu as pltpu
from jax.sharding import PartitionSpec as P

GROUP_AXES = ("outer", "rows")
HI = lax.Precision.HIGHEST
N = 1024
NB = 128
SUB = 8


def mm(a, b):
    return lax.dot_general(a, b, (((1,), (0,)), ((), ())), precision=HI, preferred_element_type=jnp.float32)


def mm_tn(a, b):
    return lax.dot_general(a, b, (((0,), (0,)), ((), ())), precision=HI, preferred_element_type=jnp.float32)


def mm_nt(a, b):
    return lax.dot_general(a, b, (((1,), (1,)), ((), ())), precision=HI, preferred_element_type=jnp.float32)


def lane(v, c):
    return jnp.broadcast_to(v[:, c:c + 1], (SUB, NB))


def factor_diag(s_ref):
    groups = NB // SUB
    for g in range(groups):
        base = SUB * g
        t = []
        for i in range(SUB):
            t.append([jnp.broadcast_to(s_ref[base + i:base + i + 1, h * NB:(h + 1) * NB], (SUB, NB)) for h in range(2)])
        a = {}
        for i in range(SUB):
            for j in range(i, SUB):
                a[i, j] = lane(t[i][0], base + j)
        inv = []
        u = {}
        rows = []
        for j in range(SUB):
            rs = lax.rsqrt(a[j, j])
            inv.append(rs)
            for i in range(j + 1, SUB):
                u[j, i] = a[j, i] * rs
            for i in range(j + 1, SUB):
                for i2 in range(i, SUB):
                    a[i, i2] = a[i, i2] - u[j, i] * u[j, i2]
            row = [t[j][h] * rs for h in range(2)]
            rows.append(row)
            for i in range(j + 1, SUB):
                for h in range(2):
                    t[i][h] = t[i][h] - u[j, i] * row[h]
        for j in range(SUB):
            for h in range(2):
                s_ref[base + j:base + j + 1, h * NB:(h + 1) * NB] = rows[j][h][0:1, :]
        for r in range(g + 1, groups):
            blk = [s_ref[SUB * r:SUB * r + SUB, h * NB:(h + 1) * NB] for h in range(2)]
            v = [lane(blk[0], base + j) for j in range(SUB)]
            for j in range(SUB):
                m = v[j] * inv[j]
                for j2 in range(j + 1, SUB):
                    v[j2] = v[j2] - m * u[j, j2]
                for h in range(2):
                    blk[h] = blk[h] - m * rows[j][h]
            for h in range(2):
                s_ref[SUB * r:SUB * r + SUB, h * NB:(h + 1) * NB] = blk[h]


PB = 256
NP = N // PB


def ds(i, n):
    return pl.ds(pl.multiple_of(i * n, n), n)


def loop(lo, hi, body):
    def step(i, carry):
        body(i)
        return carry
    lax.fori_loop(lo, hi, step, 0)


def tri_iota():
    r = lax.broadcasted_iota(jnp.int32, (NB, NB), 0)
    c = lax.broadcasted_iota(jnp.int32, (NB, NB), 1)
    return r, c


def sweep_body(w_ref, q_ref, s_ref, inv_ref):
    r, c = tri_iota()

    def panel(p):
        def half(h):
            k = 2 * p + h
            rows = ds(k, NB)
            s_ref[:, :NB] = w_ref[rows, rows]
            s_ref[:, NB:] = jnp.where(r == c, 1.0, 0.0).astype(jnp.float32)
            factor_diag(s_ref)
            w_ref[rows, rows] = jnp.where(c >= r, s_ref[:, :NB], 0.0)
            li = s_ref[:, NB:]
            inv_ref[pl.ds(pl.multiple_of(h * NB, NB), NB), pl.ds(pl.multiple_of(h * NB, NB), NB)] = li
            loop(k + 1, N // NB, lambda j: w_ref.__setitem__((rows, ds(j, NB)), mm(li, w_ref[rows, ds(j, NB)])))

            @pl.when(h == 0)
            def _():
                nxt = ds(k + 1, NB)
                lhs = w_ref[rows, nxt]
                def upd(j):
                    w_ref[nxt, ds(j, NB)] = w_ref[nxt, ds(j, NB)] - mm_tn(lhs, w_ref[rows, ds(j, NB)])
                loop(k + 1, N // NB, upd)

        loop(0, 2, half)
        pr = ds(p, PB)
        i0 = inv_ref[:NB, :NB]
        i1 = inv_ref[NB:, NB:]
        u01 = w_ref[ds(2 * p, NB), ds(2 * p + 1, NB)]
        inv_ref[NB:, :NB] = -mm(i1, mm_tn(u01, i0))
        inv_ref[:NB, NB:] = jnp.zeros((NB, NB), jnp.float32)

        def trail(i):
            def cols(j):
                w_ref[ds(i, PB), ds(j, PB)] = w_ref[ds(i, PB), ds(j, PB)] - mm_tn(w_ref[pr, ds(i, PB)], w_ref[pr, ds(j, PB)])
            loop(i, NP, cols)
        loop(p + 1, NP, trail)

        def chunk(m):
            rr = ds(m, PB)
            def prev(t):
                q_ref[rr, pr] = q_ref[rr, pr] - mm(q_ref[rr, ds(t, PB)], w_ref[ds(t, PB), pr])
            loop(0, p, prev)
            q_ref[rr, pr] = mm_nt(q_ref[rr, pr], inv_ref[...])
        loop(0, N // PB, chunk)

    loop(0, NP, panel)

    def zero(k):
        def zz(j):
            w_ref[ds(k, NB), ds(j, NB)] = jnp.zeros((NB, NB), jnp.float32)
        loop(0, k, zz)
    loop(1, N // NB, zero)


def tri_index(i, j):
    return i * NP - (i * (i - 1)) // 2 + j - i


NTRI = NP * (NP + 1) // 2


def gram_kernel(a_ref, g_ref):
    def bi(i):
        def bj(j):
            g_ref[tri_index(i, j)] = mm_tn(a_ref[:, ds(i, PB)], a_ref[:, ds(j, PB)])
        loop(i, NP, bj)
    loop(0, NP, bi)


def unpack(g_ref, u_ref):
    for i in range(NP):
        for j in range(i, NP):
            u_ref[i * PB:(i + 1) * PB, j * PB:(j + 1) * PB] = g_ref[tri_index(i, j)]


def first_kernel(g_ref, b_ref, u_ref, q_ref, s_ref, inv_ref):
    unpack(g_ref, u_ref)
    q_ref[...] = b_ref[...]
    sweep_body(u_ref, q_ref, s_ref, inv_ref)


def second_kernel(g_ref, b_ref, u1_ref, r_ref, q_ref, u_ref, s_ref, inv_ref):
    unpack(g_ref, u_ref)
    q_ref[...] = b_ref[...]
    sweep_body(u_ref, q_ref, s_ref, inv_ref)
    r_ref[...] = jnp.zeros((N, N), jnp.float32)

    def ri(i):
        def rj(j):
            def rk(k):
                r_ref[ds(i, PB), ds(j, PB)] = r_ref[ds(i, PB), ds(j, PB)] + mm(u_ref[ds(i, PB), ds(k, PB)], u1_ref[ds(k, PB), ds(j, PB)])
            loop(i, j + 1, rk)
        loop(i, NP, rj)
    loop(0, NP, ri)


VM = pl.BlockSpec(memory_space=pltpu.VMEM)
SQ = jax.ShapeDtypeStruct((N, N), jnp.float32)
PARAMS = pltpu.CompilerParams(vmem_limit_bytes=60 * 1024 * 1024)
WORK = [pltpu.VMEM((NB, 2 * NB), jnp.float32), pltpu.VMEM((PB, PB), jnp.float32)]


def gram(a):
    return pl.pallas_call(gram_kernel, out_shape=jax.ShapeDtypeStruct((NTRI, PB, PB), jnp.float32), in_specs=[VM], out_specs=VM, compiler_params=PARAMS)(a)


def first_sweep(g, a):
    return pl.pallas_call(first_kernel, out_shape=[SQ, SQ], in_specs=[VM] * 2, out_specs=[VM] * 2, scratch_shapes=WORK, compiler_params=PARAMS)(g, a)


def second_sweep(g, q, u1):
    return pl.pallas_call(second_kernel, out_shape=[SQ, SQ], in_specs=[VM] * 3, out_specs=[VM] * 2, scratch_shapes=[pltpu.VMEM((N, N), jnp.float32)] + WORK, compiler_params=PARAMS)(g, q, u1)


def solution(mesh):
    row_spec = P(("batch", "outer", "rows"), None)

    def group_qr(a_block):
        u1, q1 = first_sweep(lax.psum(gram(a_block), GROUP_AXES), a_block)
        r_block, q_block = second_sweep(lax.psum(gram(q1), GROUP_AXES), q1, u1)
        return q_block, r_block

    return jax.shard_map(group_qr, mesh=mesh, in_specs=(row_spec,), out_specs=(row_spec, P("batch", None)), check_vma=False)
```

time: 1130 us -> 492 us (0.44)
  other arithmetic: 529 us -> 0 us
  matrix products: 173 us -> 0 us
  Pallas kernels: 0 us -> 170 us
  local copies, waits for them, and re-layouts: 79.9 us -> 0 us
    another operation x66 -> x0, other arithmetic: 520 us -> none  [the longest x31 179 us: group_qr(): chol_two = jnp.linalg.cholesky(lax.psum(gram_of(q_first), GROUP_AXES))]
    pallas_call x0 -> x4, Pallas kernels: none -> 170 us  [the longest x1 74.1 us: second_sweep(): pl.pallas_call(second_kernel, out_shape=[SQ, SQ], in_specs=[VM] * 3, out_...]
    another operation x58 -> x0, matrix products: 120 us -> none  [the longest x30 71 us: right_solve(): lax.linalg.triangular_solve(chol_low, block, left_side=False, lower=True,...]
    another operation x67 -> x0, local copies, waits for them, and re-layouts: 58.5 us -> none  [the longest x51 52.8 us: right_solve(): lax.linalg.triangular_solve(chol_low, block, left_side=False, lower=True,...]
    dot_general x3 -> x0, matrix products: 52.8 us -> none  [the longest x2 32.9 us: gram_of(): lax.dot_general(block, block, (((0,), (0,)), ((), ())), precision=PRECISI...]
where the time goes in v1:
time: 492 us; the launch traced here: 491 us
  waiting for transfers between devices  307 us (62%)
  Pallas kernels  170 us (35%)
  between operations  14 us (3%)
    psum x1, waiting for transfers between devices, group_qr(): u1, q1 = first_sweep(lax.psum(gram(a_block), GROUP_AXES), a_block)  156 us
    psum x1, waiting for transfers between devices, group_qr(): r_block, q_block = second_sweep(lax.psum(gram(q1), GROUP_AXES), q1, u1)  151 us
    pallas_call x1, Pallas kernels, second_sweep(): pl.pallas_call(second_kernel, out_shape=[SQ, SQ], in_specs=[VM] * 3, out_...  74.1 us
    pallas_call x1, Pallas kernels, first_sweep(): pl.pallas_call(first_kernel, out_shape=[SQ, SQ], in_specs=[VM] * 2, out_s...  64.8 us
    pallas_call x2, Pallas kernels, gram(): pl.pallas_call(gram_kernel, out_shape=jax.ShapeDtypeStruct((NTRI, PB, PB)...  31.2 us
  transfers between devices with their start and end apart: 2, of which 2 were waited for; matrix products, arithmetic and copies ran while one was open for 0% of the time, Pallas kernels for 0%

profile of v1, /device:TPU:1, one launch (start us, length us, event | category | flops | bytes accessed | tf_op | source)
XLA Modules:
  0.0 491.4 jit_solution(15605891424529982235)
XLA Ops:
  7.2 0.0 all-reduce.3.cloned.1.call-start
  7.2 15.6 %shard_map.30 = f32[10,256,256]{2,1,0:T(8,128)} custom-call(f32[1024,1024]{1,0:T(8,128)} %b_ref.1), custom_call_target="tpu_custom_call" | custom-call | tf_op jit(solution)/shard_map/pallas_call | solution.py:198
  22.8 0.0 all-reduce.3.cloned.1.call-update
  22.8 0.0 all-reduce.5.cloned.1.call-start
  22.9 155.9 %all-reduce.3.cloned.1.call-done.g_ref = f32[10,256,256]{2,1,0:T(8,128)} async-done(((f32[10,256,256]{2,1,0:T(8,128)}), f32[10,256,256]{2,1,0:T(8,128)}) %all-reduce.3.cloned.1.call-update) | async-done | bytes 2621456 | tf_op jit(solution)/shard_map/psum | solution.py:213
  178.8 64.8 %shard_map.31 = (f32[1024,1024]{1,0:T(8,128)}, f32[1024,1024]{1,0:T(8,128)}) custom-call(f32[10,256,256]{2,1,0:T(8,128)} %all-reduce.3.cloned.1.call-done.g_ref, f32[1024,1024]{1,0:T(8,128)} %b_ref.1), custom_call_target="tpu_custom_call" | custom-call | tf_op jit(solution)/shard_map/pallas_call | solution.py:202
  243.6 15.6 %shard_map.32 = f32[10,256,256]{2,1,0:T(8,128)} custom-call(f32[1024,1024]{1,0:T(8,128)} %get-tuple-element.6.a_ref.b_ref), custom_call_target="tpu_custom_call" | custom-call | tf_op jit(solution)/shard_map/pallas_call | solution.py:198
  259.2 0.0 all-reduce.5.cloned.1.call-update
  259.2 151.2 %all-reduce.5.cloned.1.call-done.g_ref = f32[10,256,256]{2,1,0:T(8,128)} async-done(((f32[10,256,256]{2,1,0:T(8,128)}), f32[10,256,256]{2,1,0:T(8,128)}) %all-reduce.5.cloned.1.call-update) | async-done | bytes 2621456 | tf_op jit(solution)/shard_map/psum | solution.py:214
  410.4 74.1 %shard_map.33 = (f32[1024,1024]{1,0:T(8,128)}, f32[1024,1024]{1,0:T(8,128)}) custom-call(f32[10,256,256]{2,1,0:T(8,128)} %all-reduce.5.cloned.1.call-done.g_ref, f32[1024,1024]{1,0:T(8,128)} %get-tuple-element.6.a_ref.b_ref, f32[1024,1024]{1,0:T(8,128)} %get-tuple-element.7.u1_ref), custom_call_target="tpu_custom_call" | custom-call | tf_op jit(solution)/shard_map/pallas_call | solution.py:206
Async XLA Ops:
  7.2 171.7 %all-reduce.3.cloned.1.call-start = ((), (), s32[]{:S(2)}) async-start(), calls=%async_computation | async-start | bytes 5242880 | tf_op jit(solution)/shard_map/psum | solution.py:213
  22.8 387.6 %all-reduce.5.cloned.1.call-start = ((), (), s32[]{:S(2)}) async-start(), calls=%async_computation.1 | async-start | bytes 5242880 | tf_op jit(solution)/shard_map/psum | solution.py:214
Sparse Core Ops, SparseCore 0:
  23.0 155.8 all-reduce.2
  259.3 151.0 all-reduce.4
